TPU v7x, 32 devices: a whole 2x2x4 slice. The times are simulated.
32 devices in a mesh: grp: 4 (over y, x), row: 8 (over z, core).
Axes of the slice: x: 2, y: 2, z: 4, core: 2. Of those that a mesh axis runs over, the one named last changes fastest.
Arguments:
- blocks: bfloat16 [32, 4, 10, 256, 256], P(('grp', 'row')), may hold values from 0 to 1
- columns: int32 [32, 4, 10], P(('grp', 'row')), may hold values from -1 to 31, as said below
- factor: bfloat16 [64, 8192], P(None, ('grp', 'row')), may hold values from 0 to 0.3, as said below
Outputs:
- updated: float32 [64, 8192], P(None, ('grp', 'row'))
Inputs may be any that keep to these rules, and one draw needn't show every extreme that they name: Tile row i lies in group g = i // 8. In block h of tile row i the live slots come first and name distinct tile columns of group h (h * 8 to h * 8 + 7), none above i; block g always names i itself; blocks h > g are empty; a block holds at most 10 live slots, and -1 marks an empty slot. `factor`: entries are nonnegative.
All inputs are finite; a program needn't handle non-finite values.
Results may differ from a plain program's by a relative error of at most 0.0003.
Values may be sent and summed in bfloat16 or wider, within the bound.
No kernel may reach another device: no remote copies, remote signals or barrier semaphores. Data moves between devices by JAX's collectives and lax.ppermute only.
A program may use at most 128 MiB of HBM per device.

v0:
```python
import jax
import jax.numpy as jnp
from jax import lax
from jax.sharding import PartitionSpec as P

floor_value = 1e-06


def sweep(current, products, gram):

    def update(column, current):
        weights = lax.dynamic_index_in_dim(gram, column, 1, keepdims=False)
        fitted = jnp.dot(weights, current, precision=lax.Precision.HIGHEST)
        target = lax.dynamic_index_in_dim(products, column, 0, keepdims=False)
        present = lax.dynamic_index_in_dim(current, column, 0, keepdims=False)
        diagonal = gram[column, column]
        fresh = jnp.maximum(present + (target - fitted) / diagonal, floor_value)
        return lax.dynamic_update_index_in_dim(current, fresh, column, 0)

    return lax.fori_loop(0, current.shape[0], update, current)


def choose_rows(group_cols, group_number, rows_grp):
    offsets = group_cols - group_number * rows_grp
    positions = lax.broadcasted_iota(jnp.int32, (group_cols.shape[0], rows_grp), 1)
    return (offsets[:, None] == positions) & (group_cols >= 0)[:, None]


def lower_work(group_tiles, group_cols, group_number, group_factor, rows_grp):
    rank_count, span = group_factor.shape
    tile_size = span // rows_grp
    stacked = group_factor.reshape(rank_count, rows_grp, tile_size)
    selected = choose_rows(group_cols, group_number, rows_grp)
    fetched = jnp.einsum(
        "sn,rnt->srt", selected.astype(jnp.bfloat16), stacked, preferred_element_type=jnp.float32
    ).astype(jnp.bfloat16)
    return jnp.einsum("srv,suv->ru", fetched, group_tiles, preferred_element_type=jnp.float32)


def per_device(blocks, columns, factor):
    tiles_dev = blocks[0]
    cols_dev = columns[0]
    rank_count, tile_size = factor.shape
    rows_grp = lax.axis_size("row")
    group_count = lax.axis_size("grp")
    span = rows_grp * tile_size
    gram = lax.psum(jnp.dot(factor, factor.T, preferred_element_type=jnp.float32), ("grp", "row"))
    group_factor = lax.all_gather(factor, "row", axis=1, tiled=True)
    my_group = lax.axis_index("grp")
    slot_count = cols_dev.shape[1]
    live = (cols_dev >= 0).astype(jnp.float32)
    mirror = jnp.einsum("ru,hsuv->hsrv", factor, tiles_dev, preferred_element_type=jnp.float32)
    mirror = mirror * live[:, :, None, None]
    arrived, arrived_cols = (
        lax.all_to_all(mirror, "grp", split_axis=0, concat_axis=0, tiled=True),
        lax.all_to_all(cols_dev, "grp", split_axis=0, concat_axis=0, tiled=True),
    )
    flat_cols = arrived_cols.reshape(group_count * slot_count)
    selected = choose_rows(flat_cols, my_group, rows_grp).astype(jnp.float32)
    flat_mirror = arrived.reshape(group_count * slot_count, rank_count, tile_size)
    spread = jnp.einsum("sn,srv->rnv", selected, flat_mirror, precision=lax.Precision.HIGHEST)
    mirror_sum = lax.psum_scatter(
        spread.reshape(rank_count, span), "row", scatter_dimension=1, tiled=True
    )
    lower_sum = jnp.zeros((rank_count, tile_size), jnp.float32)
    piece = lax.all_gather(group_factor, "grp", axis=1, tiled=True)
    begin_at = jnp.int32(0)
    for offset in range(piece.shape[1] // span):
        group_number = begin_at // span + offset
        group_tiles = lax.dynamic_index_in_dim(tiles_dev, group_number, 0, keepdims=False)
        group_cols = lax.dynamic_index_in_dim(cols_dev, group_number, 0, keepdims=False)
        block_cols = lax.dynamic_slice_in_dim(piece, offset * span, span, 1)
        lower_sum = lower_sum + lower_work(
            group_tiles, group_cols, group_number, block_cols, rows_grp
        )
    products = lower_sum + mirror_sum
    return sweep(factor.astype(jnp.float32), products, gram)


def solution(mesh):
    in_specs = (
        P(("grp", "row"), None, None, None, None),
        P(("grp", "row"), None, None),
        P(None, ("grp", "row")),
    )
    out_specs = P(None, ("grp", "row"))
    return jax.shard_map(
        per_device, mesh=mesh, in_specs=in_specs, out_specs=out_specs, check_vma=False
    )
```

profile of v0, /device:TPU:0, one launch (start us, length us, event | category | flops | bytes accessed | tf_op | source)
XLA Modules:
  0.0 246.8 jit_solution(16195418602525848965)
XLA Ops:
  7.4 5.2 %all-to-all-start.1 = ((s32[4,1,10]{2,1,0:T(1,128)}), s32[4,1,10]{2,1,0:T(1,128)S(1)}, u32[]{:S(2)}, u32[]{:S(2)}) async-start(s32[4,1,10]{2,1,0:T(1,128)} %bitcast.144), calls=%async_computation.1 | async-start | bytes 4096 | tf_op jit(solution)/shard_map/all_to_all | solution.py:56
  12.6 15.7 %all_gather.6 = bf16[64,2048]{1,0:T(8,128)(2,1)} all-gather(bf16[64,256]{1,0:T(8,128)(2,1)} %param.7), channel_id=1, replica_groups=mesh['grp'=4,'row'=8] {'row'}, dimensions={1}, use_global_device_ids=true | all-gather | bytes 294912 | tf_op jit(solution)/shard_map/all_gather | solution.py:48
  28.3 0.7 convert_bitcast_fusion
  29.0 5.1 %multiply_bitcast_fusion = f32[4,10,64,256]{3,2,1,0:T(8,128)} fusion(bf16[1,4,10,256,256]{4,3,2,1,0:T(8,128)(2,1)} %param.5, f32[4,10]{1,0:T(4,128)S(1)} %convert_bitcast_fusion, bf16[64,256]{1,0:T(8,128)(2,1)} %param.7), kind=kOutput, calls=%fused_computation.10 | convolution fusion | flops 336199680 | bytes 7897248 | tf_op jit(solution)/shard_map/ru,hsuv->hsrv/dot_general | solution.py:52
  34.1 4.4 %all-to-all-start = ((f32[4,10,64,256]{3,2,1,0:T(8,128)}), f32[4,10,64,256]{3,2,1,0:T(8,128)S(1)}, u32[]{:S(2)}, u32[]{:S(2)}) async-start(f32[4,10,64,256]{3,2,1,0:T(8,128)} %multiply_bitcast_fusion), calls=%async_computation | async-start | bytes 5242880 | tf_op jit(solution)/shard_map/all_to_all | solution.py:55
  38.6 71.8 %psum.7 = f32[64,64]{1,0:T(8,128)S(1)} all-reduce(f32[64,64]{1,0:T(8,128)S(1)} %fusion.75), channel_id=1, replica_groups=mesh['grp'=4,'row'=8] {'grp','row'}, use_global_device_ids=true, to_apply=%region_0.0 | all-reduce | flops 4096 | bytes 32768 | tf_op jit(solution)/shard_map/psum | solution.py:47
  110.8 1.3 fusion.74
  112.2 1.2 convolution_convert_fusion.3
  113.3 1.1 convolution_convert_fusion.2
  114.5 2.4 fusion.4
  116.9 1.0 copy.21
  117.9 2.0 fusion.20
  120.7 1.8 fusion.41
  122.5 1.8 fusion.38
  124.4 24.2 %reduce-scatter.2.cloned.1.call-done = f32[64,256]{1,0:T(8,128)} async-done(((f32[64,2048]{1,0:T(8,128)}), f32[64,256]{1,0:T(8,128)}) %reduce-scatter.2.cloned.1.call-update) | async-done | bytes 65552 | tf_op jit(solution)/shard_map/reduce_scatter | solution.py:62
  148.6 1.8 fusion.35
  150.4 88.3 %while.13 = (s32[]{:T(128)}, f32[64,256]{1,0:T(8,128)S(1)}, f32[64,256]{1,0:T(8,128)S(1)}, f32[64,64]{0,1:T(8,128)S(1)}, s32[]{:T(128)}, /*index=5*/s32[]{:T(128)}) while((s32[]{:T(128)}, f32[64,256]{1,0:T(8,128)S(1)}, f32[64,256]{1,0:T(8,128)S(1)}, f32[64,64]{0,1:T(8,128)S(1)}, s32[]{:T(128)}, /*index=5*/s32[]{:T(128)}) %tuple.42), condition=%wide.region_3.4_spmd, body=%wide.region_2.3_spmd.sunk | while | flops 197634 | bytes 77417 | solution.py:20
  150.6 0.6 dynamic_slice.138
  151.9 0.6 dynamic_slice.138
  153.3 0.6 dynamic_slice.138
  154.7 0.6 dynamic_slice.138
  156.1 0.6 dynamic_slice.138
  157.5 0.6 dynamic_slice.138
  158.8 0.6 dynamic_slice.138
  160.2 0.6 dynamic_slice.138
  161.6 0.6 dynamic_slice.138
  163.0 0.6 dynamic_slice.138
  164.4 0.6 dynamic_slice.138
  165.7 0.6 dynamic_slice.138
  167.1 0.6 dynamic_slice.138
  168.5 0.6 dynamic_slice.138
  238.7 0.6 copy-done
  (336 shorter events, 79.3 us)
Async XLA Ops:
  7.4 26.7 %all-to-all-start.1 = ((s32[4,1,10]{2,1,0:T(1,128)}), s32[4,1,10]{2,1,0:T(1,128)S(1)}, u32[]{:S(2)}, u32[]{:S(2)}) async-start(s32[4,1,10]{2,1,0:T(1,128)} %bitcast.144), calls=%async_computation.1 | async-start | bytes 4096 | tf_op jit(solution)/shard_map/all_to_all | solution.py:56
  12.6 98.2 %all-gather.2.cloned.1.call-start = ((), (), s32[]{:S(2)}) async-start(), calls=%async_computation.3 | async-start | bytes 1310720 | tf_op jit(solution)/shard_map/all_gather | solution.py:66
  34.0 4.4 %copy-start.1 = (bf16[64,256]{1,0:T(8,128)(2,1)S(1)}, bf16[64,256]{1,0:T(8,128)(2,1)}, u32[]{:S(2)}) copy-start(bf16[64,256]{1,0:T(8,128)(2,1)} %param.7) | copy-start | bytes 98308
  34.0 76.4 %copy-start.3 = (s32[1,4,10]{2,1,0:T(4,128)S(1)}, s32[1,4,10]{2,1,0:T(4,128)}, u32[]{:S(2)}) copy-start(s32[1,4,10]{2,1,0:T(4,128)} %param.6) | copy-start | bytes 484
  34.1 80.4 %all-to-all-start = ((f32[4,10,64,256]{3,2,1,0:T(8,128)}), f32[4,10,64,256]{3,2,1,0:T(8,128)S(1)}, u32[]{:S(2)}, u32[]{:S(2)}) async-start(f32[4,10,64,256]{3,2,1,0:T(8,128)} %multiply_bitcast_fusion), calls=%async_computation | async-start | bytes 5242880 | tf_op jit(solution)/shard_map/all_to_all | solution.py:55
  38.4 110.1 %reduce-scatter.2.cloned.1.call-start = ((), (), s32[]{:S(2)}) async-start(), calls=%async_computation.4 | async-start | bytes 589824 | tf_op jit(solution)/shard_map/reduce_scatter | solution.py:62
  117.8 2.9 %copy-start.2 = (bf16[10,64,256]{2,0,1:T(8,128)(2,1)S(1)}, bf16[10,64,256]{2,0,1:T(8,128)(2,1)}, u32[]{:S(2)}) copy-start(bf16[10,64,256]{2,0,1:T(8,128)(2,1)} %convolution_convert_fusion.2) | copy-start | bytes 983044
  238.7 0.6 copy-start
Sparse Core Ops, SparseCore 0:
  28.4 48.7 all-gather.1
Sparse Core Ops, SparseCore 1:
  117.9 30.6 reduce-scatter.1
where the time goes:
time: 248 us; the launch traced here: 247 us
  blocking collectives  87.5 us (35%)
  local copies, waits for them, and re-layouts  44.1 us (18%)
  other arithmetic  36.8 us (15%)
  matrix products  27.2 us (11%)
  waiting for transfers between devices  24.2 us (10%)
  between operations  15 us (6%)
  starting transfers between devices  9.57 us (4%)
    psum x1, blocking collectives, per_device(): lax.psum(jnp.dot(factor, factor.T, preferred_element_type=jnp.float32), (...  71.8 us
    dynamic_slice x64, local copies, waits for them, and re-layouts, update(): diagonal = gram[column, column]  37.4 us
    max x64, other arithmetic, update(): fresh = jnp.maximum(present + (target - fitted) / diagonal, floor_value)  36.1 us
    reduce_scatter x1, waiting for transfers between devices, per_device(): lax.psum_scatter(spread.reshape(rank_count, span), 'row', scatter_dimensi...  24.2 us
    all_gather x1, blocking collectives, per_device(): group_factor = lax.all_gather(factor, 'row', axis=1, tiled=True)  15.7 us
    dot_general x64, matrix products, update(): fitted = jnp.dot(weights, current, precision=lax.Precision.HIGHEST)  9.16 us
    dot_general x4, matrix products, lower_work(): jnp.einsum('srv,suv->ru', fetched, group_tiles, preferred_element_type=jn...  7.5 us
    all_to_all x1, starting transfers between devices, per_device(): lax.all_to_all(cols_dev, 'grp', split_axis=0, concat_axis=0, tiled=True)  5.19 us
  transfers between devices with their start and end apart: 4, of which 1 were waited for; matrix products, arithmetic and copies ran while one was open for 7% of the time, Pallas kernels for 0%

commit v1 on v0

--- a/solution.py
+++ b/solution.py
@@ -44,7 +44,12 @@
     rows_grp = lax.axis_size("row")
     group_count = lax.axis_size("grp")
     span = rows_grp * tile_size
-    gram = lax.psum(jnp.dot(factor, factor.T, preferred_element_type=jnp.float32), ("grp", "row"))
+    gram = jnp.sum(
+        lax.all_gather(
+            jnp.dot(factor, factor.T, preferred_element_type=jnp.float32), ("grp", "row")
+        ),
+        axis=0,
+    )
     group_factor = lax.all_gather(factor, "row", axis=1, tiled=True)
     my_group = lax.axis_index("grp")
     slot_count = cols_dev.shape[1]

time: 248 us -> 224 us (0.903)
  blocking collectives: 87.5 us -> 65.4 us
  waiting for transfers between devices: 24.2 us -> 21 us
    psum x1 -> x0, blocking collectives: 71.8 us -> none  [per_device(): lax.psum(jnp.dot(factor, factor.T, preferred_element_type=jnp.float32), (...]
    all_gather x0 -> x1, blocking collectives: none -> 49.7 us  [per_device(): lax.all_gather(jnp.dot(factor, factor.T, preferred_element_type=jnp.float...]
    reduce_scatter x1, waiting for transfers between devices: 24.2 us -> 21 us  [per_device(): lax.psum_scatter(spread.reshape(rank_count, span), 'row', scatter_dimensi...]
  transfers between devices with their start and end apart: 4 -> 4, of which waited for: 1 -> 1; matrix products, arithmetic and copies ran while one was open for 7% -> 8% of each run, Pallas kernels for 0% -> 0%
where the time goes in v1:
time: 224 us; the launch traced here: 223 us
  blocking collectives  65.4 us (29%)
  local copies, waits for them, and re-layouts  44.1 us (20%)
  other arithmetic  38.1 us (17%)
  matrix products  27.2 us (12%)
  waiting for transfers between devices  21 us (9%)
  between operations  15 us (7%)
  starting transfers between devices  9.57 us (4%)
  loops' own time  2.29 us (1%)
    all_gather x1, blocking collectives, per_device(): lax.all_gather(jnp.dot(factor, factor.T, preferred_element_type=jnp.float...  49.7 us
    dynamic_slice x64, local copies, waits for them, and re-layouts, update(): diagonal = gram[column, column]  37.4 us
    max x64, other arithmetic, update(): fresh = jnp.maximum(present + (target - fitted) / diagonal, floor_value)  36.1 us
    reduce_scatter x1, waiting for transfers between devices, per_device(): lax.psum_scatter(spread.reshape(rank_count, span), 'row', scatter_dimensi...  21 us
    all_gather x1, blocking collectives, per_device(): group_factor = lax.all_gather(factor, 'row', axis=1, tiled=True)  15.7 us
    dot_general x64, matrix products, update(): fitted = jnp.dot(weights, current, precision=lax.Precision.HIGHEST)  9.16 us
    dot_general x4, matrix products, lower_work(): jnp.einsum('srv,suv->ru', fetched, group_tiles, preferred_element_type=jn...  7.48 us
    all_to_all x1, starting transfers between devices, per_device(): lax.all_to_all(cols_dev, 'grp', split_axis=0, concat_axis=0, tiled=True)  5.19 us
  transfers between devices with their start and end apart: 4, of which 1 were waited for; matrix products, arithmetic and copies ran while one was open for 8% of the time, Pallas kernels for 0%

profile of v1, /device:TPU:0, one launch (start us, length us, event | category | flops | bytes accessed | tf_op | source)
XLA Modules:
  0.0 222.7 jit_solution(15885760792799633113)
XLA Ops:
  7.4 5.2 %all-to-all-start.1 = ((s32[4,1,10]{2,1,0:T(1,128)}), s32[4,1,10]{2,1,0:T(1,128)S(1)}, u32[]{:S(2)}, u32[]{:S(2)}) async-start(s32[4,1,10]{2,1,0:T(1,128)} %bitcast.146), calls=%async_computation.1 | async-start | bytes 4096 | tf_op jit(solution)/shard_map/all_to_all | solution.py:61
  12.6 15.7 %all_gather.12 = bf16[64,2048]{1,0:T(8,128)(2,1)} all-gather(bf16[64,256]{1,0:T(8,128)(2,1)} %param.7), channel_id=1, replica_groups=mesh['grp'=4,'row'=8] {'row'}, dimensions={1}, use_global_device_ids=true | all-gather | bytes 294912 | tf_op jit(solution)/shard_map/all_gather | solution.py:53
  28.3 0.7 convert_bitcast_fusion
  29.0 5.1 %multiply_bitcast_fusion = f32[4,10,64,256]{3,2,1,0:T(8,128)} fusion(bf16[1,4,10,256,256]{4,3,2,1,0:T(8,128)(2,1)} %param.5, f32[4,10]{1,0:T(4,128)S(1)} %convert_bitcast_fusion, bf16[64,256]{1,0:T(8,128)(2,1)} %param.7), kind=kOutput, calls=%fused_computation.10 | convolution fusion | flops 336199680 | bytes 7897248 | tf_op jit(solution)/shard_map/ru,hsuv->hsrv/dot_general | solution.py:57
  34.2 4.4 %all-to-all-start = ((f32[4,10,64,256]{3,2,1,0:T(8,128)}), f32[4,10,64,256]{3,2,1,0:T(8,128)S(1)}, u32[]{:S(2)}, u32[]{:S(2)}) async-start(f32[4,10,64,256]{3,2,1,0:T(8,128)} %multiply_bitcast_fusion), calls=%async_computation | async-start | bytes 5242880 | tf_op jit(solution)/shard_map/all_to_all | solution.py:60
  38.6 49.7 %all-gather = f32[2048,64]{1,0:T(8,128)} all-gather(f32[64,64]{1,0:T(8,128)S(1)} %fusion.75), channel_id=2, replica_groups=mesh['grp'=4,'row'=8] {'grp','row'}, dimensions={0}, use_global_device_ids=true | all-gather | bytes 540672 | tf_op jit(solution)/shard_map/all_gather | solution.py:48
  88.2 1.3 reduce_sum.9
  89.9 1.3 fusion.74
  91.3 1.2 convolution_convert_fusion.3
  92.5 1.1 convolution_convert_fusion.2
  93.6 2.4 %fusion.4 = f32[64,256,8]{1,2,0:T(8,128)S(1)} fusion(f32[40,64,256]{2,1,0:T(8,128)S(1)} %bitcast.130, s32[40]{0:T(128)S(1)} %sub.63, pred[40]{0:T(512)(128)(4,1)S(1)} %ge.72), kind=kOutput, calls=%fused_computation.8 | convolution fusion | flops 62915200 | bytes 3145928 | tf_op jit(solution)/shard_map/sn,srv->rnv/dot_general | solution.py:66
  96.0 1.0 copy.20
  97.0 2.0 fusion.20
  99.9 1.8 fusion.41
  101.7 1.8 fusion.38
  103.5 21.0 %reduce-scatter.2.cloned.1.call-done = f32[64,256]{1,0:T(8,128)} async-done(((f32[64,2048]{1,0:T(8,128)}), f32[64,256]{1,0:T(8,128)}) %reduce-scatter.2.cloned.1.call-update) | async-done | bytes 65552 | tf_op jit(solution)/shard_map/reduce_scatter | solution.py:67
  124.5 1.8 fusion.35
  126.3 88.3 %while.13 = (s32[]{:T(128)}, f32[64,256]{1,0:T(8,128)S(1)}, f32[64,256]{1,0:T(8,128)S(1)}, f32[64,64]{0,1:T(8,128)S(1)}, s32[]{:T(128)}, /*index=5*/s32[]{:T(128)}) while((s32[]{:T(128)}, f32[64,256]{1,0:T(8,128)S(1)}, f32[64,256]{1,0:T(8,128)S(1)}, f32[64,64]{0,1:T(8,128)S(1)}, s32[]{:T(128)}, /*index=5*/s32[]{:T(128)}) %tuple.41), condition=%wide.region_3.4_spmd, body=%wide.region_2.3_spmd.sunk | while | flops 197634 | bytes 77417 | solution.py:20
  126.5 0.6 dynamic_slice.138
  127.9 0.6 dynamic_slice.138
  129.2 0.6 dynamic_slice.138
  130.6 0.6 dynamic_slice.138
  132.0 0.6 dynamic_slice.138
  133.4 0.6 dynamic_slice.138
  134.8 0.6 dynamic_slice.138
  136.1 0.6 dynamic_slice.138
  137.5 0.6 dynamic_slice.138
  138.9 0.6 dynamic_slice.138
  140.3 0.6 dynamic_slice.138
  141.7 0.6 dynamic_slice.138
  143.0 0.6 dynamic_slice.138
  214.6 0.6 copy-done
  (337 shorter events, 79.8 us)
Async XLA Ops:
  7.4 26.8 %all-to-all-start.1 = ((s32[4,1,10]{2,1,0:T(1,128)}), s32[4,1,10]{2,1,0:T(1,128)S(1)}, u32[]{:S(2)}, u32[]{:S(2)}) async-start(s32[4,1,10]{2,1,0:T(1,128)} %bitcast.146), calls=%async_computation.1 | async-start | bytes 4096 | tf_op jit(solution)/shard_map/all_to_all | solution.py:61
  12.6 77.3 %all-gather.3.cloned.1.call-start = ((), (), s32[]{:S(2)}) async-start(), calls=%async_computation.3 | async-start | bytes 1310720 | tf_op jit(solution)/shard_map/all_gather | solution.py:71
  29.0 5.1 %copy-start.1 = (bf16[64,256]{1,0:T(8,128)(2,1)S(1)}, bf16[64,256]{1,0:T(8,128)(2,1)}, u32[]{:S(2)}) copy-start(bf16[64,256]{1,0:T(8,128)(2,1)} %param.7) | copy-start | bytes 98308
  34.2 55.5 %copy-start.3 = (s32[1,4,10]{2,1,0:T(4,128)S(1)}, s32[1,4,10]{2,1,0:T(4,128)}, u32[]{:S(2)}) copy-start(s32[1,4,10]{2,1,0:T(4,128)} %param.6) | copy-start | bytes 484
  34.2 59.4 %all-to-all-start = ((f32[4,10,64,256]{3,2,1,0:T(8,128)}), f32[4,10,64,256]{3,2,1,0:T(8,128)S(1)}, u32[]{:S(2)}, u32[]{:S(2)}) async-start(f32[4,10,64,256]{3,2,1,0:T(8,128)} %multiply_bitcast_fusion), calls=%async_computation | async-start | bytes 5242880 | tf_op jit(solution)/shard_map/all_to_all | solution.py:60
  38.6 85.9 %reduce-scatter.2.cloned.1.call-start = ((), (), s32[]{:S(2)}) async-start(), calls=%async_computation.4 | async-start | bytes 589824 | tf_op jit(solution)/shard_map/reduce_scatter | solution.py:67
  97.0 2.9 %copy-start.2 = (bf16[10,64,256]{2,0,1:T(8,128)(2,1)S(1)}, bf16[10,64,256]{2,0,1:T(8,128)(2,1)}, u32[]{:S(2)}) copy-start(bf16[10,64,256]{2,0,1:T(8,128)(2,1)} %convolution_convert_fusion.2) | copy-start | bytes 983044
  214.6 0.6 copy-start
Sparse Core Ops, SparseCore 0:
  28.4 51.0 all-gather.2
Sparse Core Ops, SparseCore 1:
  97.1 27.4 reduce-scatter.1
